TPU v7x, 128 devices: a whole 4x4x4 slice. The times are simulated.
128 devices in a mesh: rows: 32 (over x, y, core), cores: 4 (over z).
Axes of the slice: x: 4, y: 4, z: 4, core: 2. Of those that a mesh axis runs over, the one named last changes fastest.
Arguments:
- rhs: float32 [524288, 128], P(('rows', 'cores')), may hold values from -6 to 6
- guess: float32 [524288, 128], P(('rows', 'cores')), may hold values from -4 to 4
- degree: float32 [524288], P(('rows', 'cores')), may hold values from 2 to 6
- weights: bfloat16 [4096, 16, 128, 128], P(('rows', 'cores')), may hold values from -0.1875 to 0.1875
- columns: int32 [4096, 16], P(('rows', 'cores')), may hold values from 0 to 287, as said below
- block_counts: int32 [4096], P(('rows', 'cores')), may hold values from 8 to 16, as said below
- send_lists: int32 [128, 128, 2], P(('rows', 'cores')), may hold values from 0 to 31
- aggregates: int32 [524288], P(('rows', 'cores')), may hold values from 0 to 16383
- coarse_diag: float32 [16384], replicated, may hold values from 4 to 32
Outputs:
- smoothed: float32 [524288, 128], P(('rows', 'cores'))
Inputs may be any that keep to these rules, and one draw needn't show every extreme that they name: `block_counts`: every block row has 8 or 16 live slots, and the rows of one device have exactly 320 live slots in all. `columns`: on every device, each table index from 32 up is named by at least one live slot.
All inputs are finite; a program needn't handle non-finite values.
Results may differ from a plain program's by a relative error of at most 0.0022.
Values may be sent and summed in bfloat16 or wider, within the bound.
A program may use at most 128 MiB of HBM per device.

v0:
```python
import jax
import jax.numpy as jnp
from jax import lax
from jax.sharding import PartitionSpec as P

NC = 16384
damping = 0.7


def body(rhs, guess, degree, weights, columns, block_counts, send_lists, aggregates, coarse_diag):
    nblocks = weights.shape[0]
    slots = weights.shape[1]
    blocksize = weights.shape[2]
    width = rhs.shape[1]
    my_lists = send_lists[0]
    flat_live = jnp.arange(slots, dtype=jnp.int32)[None, :] < block_counts[:, None]
    live_weights = weights * flat_live.astype(jnp.bfloat16)[:, :, None, None]

    def apply(field):
        blocks = field.astype(jnp.bfloat16).reshape(nblocks, blocksize, width)
        outgoing = blocks[my_lists]
        incoming = lax.all_to_all(
            outgoing, ("rows", "cores"), split_axis=0, concat_axis=0, tiled=True
        )
        table = jnp.concatenate([blocks, incoming.reshape(-1, blocksize, width)], 0)
        offsum = jnp.einsum(
            "bsij,bsjr->bir", live_weights, table[columns], preferred_element_type=jnp.float32
        )
        return degree[:, None] * field - offsum.reshape(-1, width)

    first = guess + damping * (rhs - apply(guess)) / degree[:, None]
    residue = rhs - apply(first)
    local_coarse = jax.ops.segment_sum(residue, aggregates, num_segments=NC)
    total = lax.psum(local_coarse, ("rows", "cores"))
    correction = (total / coarse_diag[:, None]).astype(jnp.bfloat16)
    second = first + correction[aggregates].astype(jnp.float32)
    return second + damping * (rhs - apply(second)) / degree[:, None]


def solution(mesh):
    return jax.shard_map(
        body,
        mesh=mesh,
        in_specs=(
            P(("rows", "cores"), None),
            P(("rows", "cores"), None),
            P(("rows", "cores")),
            P(("rows", "cores"), None, None, None),
            P(("rows", "cores"), None),
            P(("rows", "cores")),
            P(("rows", "cores"), None, None),
            P(("rows", "cores")),
            P(),
        ),
        out_specs=P(("rows", "cores"), None),
        check_vma=False,
    )
```

profile of v0, /device:TPU:1, one launch (start us, length us, event | category | flops | bytes accessed | tf_op | source)
XLA Modules:
  0.0 701.2 jit_solution(10539362851413579965)
XLA Ops:
  6.5 0.7 compare_select_fusion.2
  7.2 0.1 copy.10
  7.3 0.1 reshape.90
  7.5 1.7 convert_element_type.23
  9.2 8.6 %gather_fusion = bf16[256,128,128]{2,1,0:T(8,128)(2,1)} fusion(bf16[32,128,128]{2,1,0:T(8,128)(2,1)S(1)} %bitcast.53, s32[1024]{0:T(1024)S(1)} %pad_clamp_fusion.1), kind=kCustom, calls=%fused_computation | custom fusion | bytes 16778240 | tf_op jit(solution)/shard_map/gather | solution.py:21
  17.8 0.0 copy-start.8
  17.8 0.0 copy-start.9
  17.8 12.0 %all-to-all-start = ((bf16[128,2,128,128]{3,2,1,0:T(8,128)(2,1)}), bf16[128,2,128,128]{3,2,1,0:T(8,128)(2,1)}, u32[]{:S(2)}, u32[]{:S(2)}) async-start(bf16[128,2,128,128]{3,2,1,0:T(8,128)(2,1)} %bitcast.59), calls=%async_computation | async-start | bytes 16777216 | tf_op jit(solution)/shard_map/all_to_all | solution.py:22
  29.8 0.2 all-reduce.2.cloned.1.call-start
  30.0 0.0 copy-done.8
  30.0 0.1 copy.11
  30.1 0.1 reshape.98
  30.2 0.0 copy-done.9
  30.2 0.1 fusion.22
  30.3 100.4 %all-to-all-done = bf16[128,2,128,128]{3,2,1,0:T(8,128)(2,1)} async-done(((bf16[128,2,128,128]{3,2,1,0:T(8,128)(2,1)}), bf16[128,2,128,128]{3,2,1,0:T(8,128)(2,1)}, u32[]{:S(2)}, u32[]{:S(2)}) %all-to-all-start) | async-done | bytes 8388640 | tf_op jit(solution)/shard_map/all_to_all | solution.py:22
  130.7 7.8 %pad_maximum_fusion = bf16[288,128,128]{2,1,0:T(8,128)(2,1)} fusion(bf16[256,128,128]{2,1,0:T(8,128)(2,1)} %bitcast.3, bf16[32,128,128]{2,1,0:T(8,128)(2,1)S(1)} %bitcast.54), kind=kLoop, calls=%fused_computation.14 | loop fusion | flops 4718592 | bytes 18874368 | tf_op jit(solution)/shard_map/concatenate | solution.py:25
  138.5 17.6 %gather_fusion.1 = bf16[512,128,128]{2,1,0:T(8,128)(2,1)} fusion(bf16[288,128,128]{2,1,0:T(8,128)(2,1)} %pad_maximum_fusion, s32[1024]{0:T(1024)S(1)} %pad_clamp_fusion), kind=kCustom, calls=%fused_computation.1 | custom fusion | bytes 33556480 | tf_op jit(solution)/shard_map/gather | solution.py:27
  156.1 0.0 copy-start
  156.1 0.0 copy-start.4
  156.1 13.1 %fusion.4 = f32[32,128,128,1]{2,1,3,0:T(8,128)S(1)} fusion(bf16[32,16,128,128]{3,2,1,0:T(8,128)(2,1)} %bitcast.65, bf16[32,16,128,128]{3,2,1,0:T(8,128)(2,1)} %param.12, bf16[32,16]{1,0:T(8,128)(2,1)S(1)} %fusion.22), kind=kOutput, calls=%fused_computation.12 | convolution fusion | flops 2155872256 | bytes 35652608 | tf_op jit(solution)/shard_map/bsij,bsjr->bir/dot_general | solution.py:26
  169.2 0.0 copy-done
  169.2 0.0 copy-done.4
  169.2 0.0 copy-done.5
  169.3 1.0 fusion.23
  170.3 8.6 %gather_fusion.2 = bf16[256,128,128]{2,1,0:T(8,128)(2,1)} fusion(bf16[32,128,128]{2,1,0:T(8,128)(2,1)S(1)} %bitcast.55, s32[1024]{0:T(1024)S(1)} %pad_clamp_fusion.1), kind=kCustom, calls=%fused_computation.2 | custom fusion | bytes 16778240 | tf_op jit(solution)/shard_map/gather | solution.py:21
  178.9 111.8 %all_to_all.15 = bf16[128,2,128,128]{3,2,1,0:T(8,128)(2,1)} all-to-all(bf16[128,2,128,128]{3,2,1,0:T(8,128)(2,1)} %bitcast.63), channel_id=1, replica_groups=mesh['rows'=32,'cores'=4] {'rows','cores'}, dimensions={0} | all-to-all | bytes 16777216 | tf_op jit(solution)/shard_map/all_to_all | solution.py:22
  290.8 7.8 %pad_maximum_fusion.1 = bf16[288,128,128]{2,1,0:T(8,128)(2,1)} fusion(bf16[256,128,128]{2,1,0:T(8,128)(2,1)} %bitcast.60, bf16[32,128,128]{2,1,0:T(8,128)(2,1)S(1)} %bitcast.56), kind=kLoop, calls=%fused_computation.15 | loop fusion | flops 4718592 | bytes 18874368 | tf_op jit(solution)/shard_map/concatenate | solution.py:25
  298.6 17.6 %gather_fusion.3 = bf16[512,128,128]{2,1,0:T(8,128)(2,1)} fusion(bf16[288,128,128]{2,1,0:T(8,128)(2,1)} %pad_maximum_fusion.1, s32[1024]{0:T(1024)S(1)} %pad_clamp_fusion), kind=kCustom, calls=%fused_computation.3 | custom fusion | bytes 33556480 | tf_op jit(solution)/shard_map/gather | solution.py:27
  316.2 13.1 %fusion.2 = f32[32,128,128,1]{2,1,3,0:T(8,128)S(1)} fusion(bf16[32,16,128,128]{3,2,1,0:T(8,128)(2,1)} %bitcast.66, bf16[32,16,128,128]{3,2,1,0:T(8,128)(2,1)} %param.12, bf16[32,16]{1,0:T(8,128)(2,1)S(1)} %fusion.22), kind=kOutput, calls=%fused_computation.10 | convolution fusion | flops 2155872256 | bytes 35652608 | tf_op jit(solution)/shard_map/bsij,bsjr->bir/dot_general | solution.py:26
  329.3 0.0 copy-start.7
  329.3 0.0 copy-done.1
  329.3 2.0 fusion.15
  331.3 0.0 copy-done.7
  331.3 26.4 %scatter_custom_fusion = f32[16384,128]{1,0:T(8,128)} fusion(s32[4096]{0:T(1024)S(1)} %copy-done.7, f32[4096,128]{1,0:T(8,128)} %fusion.15, f32[]{:T(128)} %constant.2.clone.1), kind=kCustom, calls=%fused_computation.21 | custom fusion | flops 524288 | bytes 8389120 | tf_op jit(solution)/shard_map/scatter-add | solution.py:33
  357.7 0.0 all-reduce.2.cloned.1.call-update
  357.8 156.8 %all-reduce.2.cloned.1.call-done = f32[16384,128]{1,0:T(8,128)} async-done(((f32[16384,128]{1,0:T(8,128)}), f32[16384,128]{1,0:T(8,128)}) %all-reduce.2.cloned.1.call-update) | async-done | bytes 8388624 | tf_op jit(solution)/shard_map/psum | solution.py:34
  514.6 0.0 copy-done.6
  514.6 6.9 divide_convert_fusion
  521.5 17.1 %gather_fusion.4 = bf16[4096,128]{1,0:T(8,128)(2,1)} fusion(bf16[16384,128]{1,0:T(8,128)(2,1)} %divide_convert_fusion, s32[4096]{0:T(1024)S(1)} %fusion.21), kind=kCustom, calls=%fused_computation.4 | custom fusion | bytes 2113536 | tf_op jit(solution)/shard_map/gather | solution.py:36
  538.6 1.4 fusion.20
  540.0 8.6 %gather_fusion.5 = bf16[256,128,128]{2,1,0:T(8,128)(2,1)} fusion(bf16[32,128,128]{2,1,0:T(8,128)(2,1)S(1)} %bitcast.57, s32[1024]{0:T(1024)S(1)} %pad_clamp_fusion.1), kind=kCustom, calls=%fused_computation.5 | custom fusion | bytes 16778240 | tf_op jit(solution)/shard_map/gather | solution.py:21
  548.6 105.2 %all_to_all.16 = bf16[128,2,128,128]{3,2,1,0:T(8,128)(2,1)} all-to-all(bf16[128,2,128,128]{3,2,1,0:T(8,128)(2,1)} %bitcast.62), channel_id=1, replica_groups=mesh['rows'=32,'cores'=4] {'rows','cores'}, dimensions={0} | all-to-all | bytes 16777216 | tf_op jit(solution)/shard_map/all_to_all | solution.py:22
  653.8 7.8 %pad_maximum_fusion.2 = bf16[288,128,128]{2,1,0:T(8,128)(2,1)} fusion(bf16[256,128,128]{2,1,0:T(8,128)(2,1)} %bitcast.61, bf16[32,128,128]{2,1,0:T(8,128)(2,1)S(1)} %bitcast.58), kind=kLoop, calls=%fused_computation.16 | loop fusion | flops 4718592 | bytes 18874368 | tf_op jit(solution)/shard_map/concatenate | solution.py:25
  661.6 17.6 %gather_fusion.6 = bf16[512,128,128]{2,1,0:T(8,128)(2,1)} fusion(bf16[288,128,128]{2,1,0:T(8,128)(2,1)} %pad_maximum_fusion.2, s32[1024]{0:T(1024)S(1)} %pad_clamp_fusion), kind=kCustom, calls=%fused_computation.6 | custom fusion | bytes 33556480 | tf_op jit(solution)/shard_map/gather | solution.py:27
  679.2 13.1 %fusion = f32[32,128,128,1]{2,1,3,0:T(8,128)S(1)} fusion(bf16[32,16,128,128]{3,2,1,0:T(8,128)(2,1)} %bitcast.64, bf16[32,16,128,128]{3,2,1,0:T(8,128)(2,1)} %param.12, bf16[32,16]{1,0:T(8,128)(2,1)S(1)} %fusion.22), kind=kOutput, calls=%fused_computation.8 | convolution fusion | flops 2155872256 | bytes 35652608 | tf_op jit(solution)/shard_map/bsij,bsjr->bir/dot_general | solution.py:26
  692.4 0.0 copy-done.2
  692.4 0.0 copy-done.3
  692.4 2.0 fusion.14
  (9 shorter events, 0.0 us)
Async XLA Ops:
  17.8 12.2 %copy-start.8 = (s32[32,16]{0,1:T(8,128)S(1)}, s32[32,16]{0,1:T(8,128)}, u32[]{:S(2)}) copy-start(s32[32,16]{0,1:T(8,128)} %param.13) | copy-start | bytes 6148
  17.8 12.4 %copy-start.9 = (s32[32]{0:T(128)S(1)}, s32[32]{0:T(128)}, u32[]{:S(2)}) copy-start(s32[32]{0:T(128)} %param.14) | copy-start | bytes 388
  17.8 112.9 %all-to-all-start = ((bf16[128,2,128,128]{3,2,1,0:T(8,128)(2,1)}), bf16[128,2,128,128]{3,2,1,0:T(8,128)(2,1)}, u32[]{:S(2)}, u32[]{:S(2)}) async-start(bf16[128,2,128,128]{3,2,1,0:T(8,128)(2,1)} %bitcast.59), calls=%async_computation | async-start | bytes 16777216 | tf_op jit(solution)/shard_map/all_to_all | solution.py:22
  29.8 484.8 %all-reduce.2.cloned.1.call-start = ((), (), s32[]{:S(2)}) async-start(), calls=%async_computation.3 | async-start | bytes 16777216 | tf_op jit(solution)/shard_map/psum | solution.py:34
  156.1 13.1 %copy-start = (f32[4096,128]{1,0:T(8,128)S(1)}, f32[4096,128]{1,0:T(8,128)}, u32[]{:S(2)}) copy-start(f32[4096,128]{1,0:T(8,128)} %param.9) | copy-start | bytes 6291460
  156.1 13.1 %copy-start.4 = (f32[4096,128]{1,0:T(8,128)S(1)}, f32[4096,128]{1,0:T(8,128)}, u32[]{:S(2)}) copy-start(f32[4096,128]{1,0:T(8,128)} %param.10) | copy-start | bytes 6291460
  156.1 13.1 %copy-start.5 = (f32[4096]{0:T(1024)S(1)}, f32[4096]{0:T(1024)}, u32[]{:S(2)}) copy-start(f32[4096]{0:T(1024)} %param.11) | copy-start | bytes 49156
  316.2 13.1 %copy-start.1 = (f32[4096,128]{1,0:T(8,128)S(1)}, f32[4096,128]{1,0:T(8,128)}, u32[]{:S(2)}) copy-start(f32[4096,128]{1,0:T(8,128)} %param.9) | copy-start | bytes 6291460
  329.3 2.0 copy-start.7
  331.3 183.3 %copy-start.6 = (f32[16384]{0:T(1024)S(1)}, f32[16384]{0:T(1024)}, u32[]{:S(2)}) copy-start(f32[16384]{0:T(1024)} %param.17) | copy-start | bytes 196612
  679.2 13.1 %copy-start.2 = (f32[4096,128]{1,0:T(8,128)S(1)}, f32[4096,128]{1,0:T(8,128)}, u32[]{:S(2)}) copy-start(f32[4096,128]{1,0:T(8,128)} %param.9) | copy-start | bytes 6291460
  679.2 13.1 %copy-start.3 = (bf16[4096,128]{1,0:T(8,128)(2,1)S(1)}, bf16[4096,128]{1,0:T(8,128)(2,1)}, u32[]{:S(2)}) copy-start(bf16[4096,128]{1,0:T(8,128)(2,1)} %gather_fusion.4) | copy-start | bytes 3145732
Sparse Core Ops, SparseCore 0:
  357.9 156.6 all-reduce.1
where the time goes:
time: 702 us; the launch traced here: 701 us
  waiting for transfers between devices  257 us (37%)
  blocking collectives  217 us (31%)
  local copies, waits for them, and re-layouts  96.2 us (14%)
  other arithmetic  65.7 us (9%)
  matrix products  39.3 us (6%)
  between operations  13.6 us (2%)
  starting transfers between devices  12.2 us (2%)
    all_to_all x2, blocking collectives, apply(): lax.all_to_all(outgoing, ('rows', 'cores'), split_axis=0, concat_axis=0,...  217 us
    psum x1, waiting for transfers between devices, body(): total = lax.psum(local_coarse, ('rows', 'cores'))  157 us
    all_to_all x1, waiting for transfers between devices, apply(): lax.all_to_all(outgoing, ('rows', 'cores'), split_axis=0, concat_axis=0,...  100 us
    gather x3, local copies, waits for them, and re-layouts, apply(): table[columns]  52.8 us
    dot_general x3, matrix products, apply(): jnp.einsum('bsij,bsjr->bir', live_weights, table[columns], preferred_elem...  39.3 us
    scatter-add x1, other arithmetic, body(): local_coarse = jax.ops.segment_sum(residue, aggregates, num_segments=NC)  26.4 us
    gather x3, local copies, waits for them, and re-layouts, apply(): outgoing = blocks[my_lists]  25.8 us
    concatenate x3, other arithmetic, apply(): table = jnp.concatenate([blocks, incoming.reshape(-1, blocksize, width)], 0)  23.5 us
  transfers between devices with their start and end apart: 2, of which 2 were waited for; matrix products, arithmetic and copies ran while one was open for 0% of the time, Pallas kernels for 0%

commit v1 on v0

--- a/solution.py
+++ b/solution.py
@@ -31,7 +31,7 @@
     first = guess + damping * (rhs - apply(guess)) / degree[:, None]
     residue = rhs - apply(first)
     local_coarse = jax.ops.segment_sum(residue, aggregates, num_segments=NC)
-    total = lax.psum(local_coarse, ("rows", "cores"))
+    total = lax.psum(lax.psum(local_coarse, "cores"), "rows")
     correction = (total / coarse_diag[:, None]).astype(jnp.bfloat16)
     second = first + correction[aggregates].astype(jnp.float32)
     return second + damping * (rhs - apply(second)) / degree[:, None]

time: 702 us -> 825 us (1.18)
  waiting for transfers between devices: 257 us -> 379 us
    psum x1 -> x2, waiting for transfers between devices: 157 us -> 279 us  [body(): total = lax.psum(lax.psum(local_coarse, 'cores'), 'rows')]
  transfers between devices with their start and end apart: 2 -> 3, of which waited for: 2 -> 3; matrix products, arithmetic and copies ran while one was open for 0% -> 0% of each run, Pallas kernels for 0% -> 0%
where the time goes in v1:
time: 825 us; the launch traced here: 824 us
  waiting for transfers between devices  379 us (46%)
  blocking collectives  218 us (26%)
  local copies, waits for them, and re-layouts  96.2 us (12%)
  other arithmetic  65.6 us (8%)
  matrix products  39.3 us (5%)
  between operations  13.6 us (2%)
  starting transfers between devices  12.5 us (2%)
    psum x2, waiting for transfers between devices, body(): total = lax.psum(lax.psum(local_coarse, 'cores'), 'rows')  279 us
    all_to_all x2, blocking collectives, apply(): lax.all_to_all(outgoing, ('rows', 'cores'), split_axis=0, concat_axis=0,...  218 us
    all_to_all x1, waiting for transfers between devices, apply(): lax.all_to_all(outgoing, ('rows', 'cores'), split_axis=0, concat_axis=0,...  100 us
    gather x3, local copies, waits for them, and re-layouts, apply(): table[columns]  52.8 us
    dot_general x3, matrix products, apply(): jnp.einsum('bsij,bsjr->bir', live_weights, table[columns], preferred_elem...  39.3 us
    scatter-add x1, other arithmetic, body(): local_coarse = jax.ops.segment_sum(residue, aggregates, num_segments=NC)  26.4 us
    gather x3, local copies, waits for them, and re-layouts, apply(): outgoing = blocks[my_lists]  25.8 us
    concatenate x3, other arithmetic, apply(): table = jnp.concatenate([blocks, incoming.reshape(-1, blocksize, width)], 0)  23.5 us
  transfers between devices with their start and end apart: 3, of which 3 were waited for; matrix products, arithmetic and copies ran while one was open for 0% of the time, Pallas kernels for 0%

profile of v1, /device:TPU:1, one launch (start us, length us, event | category | flops | bytes accessed | tf_op | source)
XLA Modules:
  0.0 824.3 jit_solution(2202250085979300078)
XLA Ops:
  6.5 0.7 compare_select_fusion.2
  7.2 0.1 copy.10
  7.3 0.1 reshape.90
  7.5 1.7 convert_element_type.23
  9.2 8.6 %gather_fusion = bf16[256,128,128]{2,1,0:T(8,128)(2,1)} fusion(bf16[32,128,128]{2,1,0:T(8,128)(2,1)S(1)} %bitcast.53, s32[1024]{0:T(1024)S(1)} %pad_clamp_fusion.1), kind=kCustom, calls=%fused_computation | custom fusion | bytes 16778240 | tf_op jit(solution)/shard_map/gather | solution.py:21
  17.8 0.0 copy-start.8
  17.8 12.0 %all-to-all-start = ((bf16[128,2,128,128]{3,2,1,0:T(8,128)(2,1)}), bf16[128,2,128,128]{3,2,1,0:T(8,128)(2,1)}, u32[]{:S(2)}, u32[]{:S(2)}) async-start(bf16[128,2,128,128]{3,2,1,0:T(8,128)(2,1)} %bitcast.59), calls=%async_computation | async-start | bytes 16777216 | tf_op jit(solution)/shard_map/all_to_all | solution.py:22
  29.8 0.2 all-reduce.3.cloned.1.call-start
  30.0 0.0 copy-done.8
  30.0 0.1 copy.11
  30.1 0.1 reshape.98
  30.2 0.0 copy-done.9
  30.2 0.1 fusion.22
  30.3 100.4 %all-to-all-done = bf16[128,2,128,128]{3,2,1,0:T(8,128)(2,1)} async-done(((bf16[128,2,128,128]{3,2,1,0:T(8,128)(2,1)}), bf16[128,2,128,128]{3,2,1,0:T(8,128)(2,1)}, u32[]{:S(2)}, u32[]{:S(2)}) %all-to-all-start) | async-done | bytes 8388640 | tf_op jit(solution)/shard_map/all_to_all | solution.py:22
  130.7 7.8 pad_maximum_fusion
  138.5 17.6 %gather_fusion.1 = bf16[512,128,128]{2,1,0:T(8,128)(2,1)} fusion(bf16[288,128,128]{2,1,0:T(8,128)(2,1)} %pad_maximum_fusion, s32[1024]{0:T(1024)S(1)} %pad_clamp_fusion), kind=kCustom, calls=%fused_computation.1 | custom fusion | bytes 33556480 | tf_op jit(solution)/shard_map/gather | solution.py:27
  156.1 13.1 %fusion.4 = f32[32,128,128,1]{2,1,3,0:T(8,128)S(1)} fusion(bf16[32,16,128,128]{3,2,1,0:T(8,128)(2,1)} %bitcast.65, bf16[32,16,128,128]{3,2,1,0:T(8,128)(2,1)} %param.12, bf16[32,16]{1,0:T(8,128)(2,1)S(1)} %fusion.22), kind=kOutput, calls=%fused_computation.12 | convolution fusion | flops 2155872256 | bytes 35652608 | tf_op jit(solution)/shard_map/bsij,bsjr->bir/dot_general | solution.py:26
  169.2 0.0 copy-done
  169.2 0.0 copy-done.4
  169.2 0.0 copy-done.5
  169.3 1.0 fusion.23
  170.3 8.6 %gather_fusion.2 = bf16[256,128,128]{2,1,0:T(8,128)(2,1)} fusion(bf16[32,128,128]{2,1,0:T(8,128)(2,1)S(1)} %bitcast.55, s32[1024]{0:T(1024)S(1)} %pad_clamp_fusion.1), kind=kCustom, calls=%fused_computation.2 | custom fusion | bytes 16778240 | tf_op jit(solution)/shard_map/gather | solution.py:21
  178.9 111.8 %all_to_all.15 = bf16[128,2,128,128]{3,2,1,0:T(8,128)(2,1)} all-to-all(bf16[128,2,128,128]{3,2,1,0:T(8,128)(2,1)} %bitcast.63), channel_id=1, replica_groups=mesh['rows'=32,'cores'=4] {'rows','cores'}, dimensions={0} | all-to-all | bytes 16777216 | tf_op jit(solution)/shard_map/all_to_all | solution.py:22
  290.8 7.8 pad_maximum_fusion.1
  298.6 17.6 %gather_fusion.3 = bf16[512,128,128]{2,1,0:T(8,128)(2,1)} fusion(bf16[288,128,128]{2,1,0:T(8,128)(2,1)} %pad_maximum_fusion.1, s32[1024]{0:T(1024)S(1)} %pad_clamp_fusion), kind=kCustom, calls=%fused_computation.3 | custom fusion | bytes 33556480 | tf_op jit(solution)/shard_map/gather | solution.py:27
  316.2 13.1 %fusion.2 = f32[32,128,128,1]{2,1,3,0:T(8,128)S(1)} fusion(bf16[32,16,128,128]{3,2,1,0:T(8,128)(2,1)} %bitcast.66, bf16[32,16,128,128]{3,2,1,0:T(8,128)(2,1)} %param.12, bf16[32,16]{1,0:T(8,128)(2,1)S(1)} %fusion.22), kind=kOutput, calls=%fused_computation.10 | convolution fusion | flops 2155872256 | bytes 35652608 | tf_op jit(solution)/shard_map/bsij,bsjr->bir/dot_general | solution.py:26
  329.3 0.0 copy-start.7
  329.3 0.0 copy-done.1
  329.3 2.0 fusion.15
  331.3 0.0 copy-done.7
  331.3 26.4 %scatter_custom_fusion = f32[16384,128]{1,0:T(8,128)} fusion(s32[4096]{0:T(1024)S(1)} %copy-done.7, f32[4096,128]{1,0:T(8,128)} %fusion.15, f32[]{:T(128)} %constant.2.clone.1), kind=kCustom, calls=%fused_computation.21 | custom fusion | flops 524288 | bytes 8389120 | tf_op jit(solution)/shard_map/scatter-add | solution.py:33
  357.7 0.0 all-reduce.3.cloned.1.call-update
  357.8 0.3 all-reduce.5.cloned.1.call-start
  358.1 155.5 %all-reduce.3.cloned.1.call-done = f32[16384,128]{1,0:T(8,128)} async-done(((f32[16384,128]{1,0:T(8,128)}), f32[16384,128]{1,0:T(8,128)}) %all-reduce.3.cloned.1.call-update) | async-done | bytes 8388624 | tf_op jit(solution)/shard_map/psum | solution.py:34
  513.6 0.0 all-reduce.5.cloned.1.call-update
  513.6 123.0 %all-reduce.5.cloned.1.call-done = f32[16384,128]{1,0:T(8,128)} async-done(((f32[16384,128]{1,0:T(8,128)}), f32[16384,128]{1,0:T(8,128)}) %all-reduce.5.cloned.1.call-update) | async-done | bytes 8388624 | tf_op jit(solution)/shard_map/psum | solution.py:34
  636.6 0.0 copy-done.6
  636.6 6.8 divide_convert_fusion
  643.5 17.1 %gather_fusion.4 = bf16[4096,128]{1,0:T(8,128)(2,1)} fusion(bf16[16384,128]{1,0:T(8,128)(2,1)} %divide_convert_fusion, s32[4096]{0:T(1024)S(1)} %fusion.21), kind=kCustom, calls=%fused_computation.4 | custom fusion | bytes 2113536 | tf_op jit(solution)/shard_map/gather | solution.py:36
  660.6 1.4 fusion.20
  662.0 8.6 %gather_fusion.5 = bf16[256,128,128]{2,1,0:T(8,128)(2,1)} fusion(bf16[32,128,128]{2,1,0:T(8,128)(2,1)S(1)} %bitcast.57, s32[1024]{0:T(1024)S(1)} %pad_clamp_fusion.1), kind=kCustom, calls=%fused_computation.5 | custom fusion | bytes 16778240 | tf_op jit(solution)/shard_map/gather | solution.py:21
  670.6 106.2 %all_to_all.16 = bf16[128,2,128,128]{3,2,1,0:T(8,128)(2,1)} all-to-all(bf16[128,2,128,128]{3,2,1,0:T(8,128)(2,1)} %bitcast.62), channel_id=1, replica_groups=mesh['rows'=32,'cores'=4] {'rows','cores'}, dimensions={0} | all-to-all | bytes 16777216 | tf_op jit(solution)/shard_map/all_to_all | solution.py:22
  776.9 7.8 pad_maximum_fusion.2
  784.7 17.6 %gather_fusion.6 = bf16[512,128,128]{2,1,0:T(8,128)(2,1)} fusion(bf16[288,128,128]{2,1,0:T(8,128)(2,1)} %pad_maximum_fusion.2, s32[1024]{0:T(1024)S(1)} %pad_clamp_fusion), kind=kCustom, calls=%fused_computation.6 | custom fusion | bytes 33556480 | tf_op jit(solution)/shard_map/gather | solution.py:27
  802.3 13.1 %fusion = f32[32,128,128,1]{2,1,3,0:T(8,128)S(1)} fusion(bf16[32,16,128,128]{3,2,1,0:T(8,128)(2,1)} %bitcast.64, bf16[32,16,128,128]{3,2,1,0:T(8,128)(2,1)} %param.12, bf16[32,16]{1,0:T(8,128)(2,1)S(1)} %fusion.22), kind=kOutput, calls=%fused_computation.8 | convolution fusion | flops 2155872256 | bytes 35652608 | tf_op jit(solution)/shard_map/bsij,bsjr->bir/dot_general | solution.py:26
  815.4 0.0 copy-done.2
  815.4 0.0 copy-done.3
  815.5 2.0 fusion.14
  (12 shorter events, 0.0 us)
Async XLA Ops:
  17.8 12.2 %copy-start.8 = (s32[32,16]{0,1:T(8,128)S(1)}, s32[32,16]{0,1:T(8,128)}, u32[]{:S(2)}) copy-start(s32[32,16]{0,1:T(8,128)} %param.13) | copy-start | bytes 6148
  17.8 12.4 %copy-start.9 = (s32[32]{0:T(128)S(1)}, s32[32]{0:T(128)}, u32[]{:S(2)}) copy-start(s32[32]{0:T(128)} %param.14) | copy-start | bytes 388
  17.8 112.9 %all-to-all-start = ((bf16[128,2,128,128]{3,2,1,0:T(8,128)(2,1)}), bf16[128,2,128,128]{3,2,1,0:T(8,128)(2,1)}, u32[]{:S(2)}, u32[]{:S(2)}) async-start(bf16[128,2,128,128]{3,2,1,0:T(8,128)(2,1)} %bitcast.59), calls=%async_computation | async-start | bytes 16777216 | tf_op jit(solution)/shard_map/all_to_all | solution.py:22
  29.8 483.8 %all-reduce.3.cloned.1.call-start = ((), (), s32[]{:S(2)}) async-start(), calls=%async_computation.3 | async-start | bytes 16777216 | tf_op jit(solution)/shard_map/psum | solution.py:34
  156.1 13.1 %copy-start = (f32[4096,128]{1,0:T(8,128)S(1)}, f32[4096,128]{1,0:T(8,128)}, u32[]{:S(2)}) copy-start(f32[4096,128]{1,0:T(8,128)} %param.9) | copy-start | bytes 6291460
  156.1 13.1 %copy-start.4 = (f32[4096,128]{1,0:T(8,128)S(1)}, f32[4096,128]{1,0:T(8,128)}, u32[]{:S(2)}) copy-start(f32[4096,128]{1,0:T(8,128)} %param.10) | copy-start | bytes 6291460
  156.1 13.1 %copy-start.5 = (f32[4096]{0:T(1024)S(1)}, f32[4096]{0:T(1024)}, u32[]{:S(2)}) copy-start(f32[4096]{0:T(1024)} %param.11) | copy-start | bytes 49156
  316.2 13.1 %copy-start.1 = (f32[4096,128]{1,0:T(8,128)S(1)}, f32[4096,128]{1,0:T(8,128)}, u32[]{:S(2)}) copy-start(f32[4096,128]{1,0:T(8,128)} %param.9) | copy-start | bytes 6291460
  329.3 2.0 copy-start.7
  357.7 278.9 %copy-start.6 = (f32[16384]{0:T(1024)S(1)}, f32[16384]{0:T(1024)}, u32[]{:S(2)}) copy-start(f32[16384]{0:T(1024)} %param.17) | copy-start | bytes 196612
  357.8 278.9 %all-reduce.5.cloned.1.call-start = ((), (), s32[]{:S(2)}) async-start(), calls=%async_computation.4 | async-start | bytes 16777216 | tf_op jit(solution)/shard_map/psum | solution.py:34
  802.3 13.1 %copy-start.2 = (f32[4096,128]{1,0:T(8,128)S(1)}, f32[4096,128]{1,0:T(8,128)}, u32[]{:S(2)}) copy-start(f32[4096,128]{1,0:T(8,128)} %param.9) | copy-start | bytes 6291460
  802.3 13.1 %copy-start.3 = (bf16[4096,128]{1,0:T(8,128)(2,1)S(1)}, bf16[4096,128]{1,0:T(8,128)(2,1)}, u32[]{:S(2)}) copy-start(bf16[4096,128]{1,0:T(8,128)(2,1)} %gather_fusion.4) | copy-start | bytes 3145732
Sparse Core Ops, SparseCore 0:
  357.9 155.6 all-reduce.2
  516.9 119.6 all-reduce.4
